TPU v7x, 128 devices: a whole 4x4x4 slice. The times are simulated.
128 devices in a mesh: section: 4 (over y), wide: 8 (over z, x_hi), narrow: 4 (over x_lo, core).
Axes of the slice: x: 4 (x_hi: 2, x_lo: 2; x = x_hi * 2 + x_lo), y: 4, z: 4, core: 2. Of those that a mesh axis runs over, the one named last changes fastest.
Arguments:
- normed_inputs: bfloat16 [4, 4, 4, 768, 4096], P('section', 'narrow', None, 'wide'), may hold values from -160 to 160
- value_cotangent: bfloat16 [4, 4, 4, 768, 1024], P('section', 'narrow', None, 'wide'), may hold values from -6 to 6
- expert_hidden: bfloat16 [4, 4, 4, 256, 7168], P('section', 'narrow', None, None, 'wide'), may hold values from -40 to 40
- expert_cotangent: bfloat16 [4, 4, 4, 256, 4096], P('section', 'narrow', None, 'wide'), may hold values from -110 to 110
- slot_gate: bfloat16 [4, 4, 4, 256], P('section', 'narrow', None, 'wide'), may hold values from 0.25 to 1
- slot_count: int32 [4, 4, 4], P('section', 'narrow'), may hold values from 129 to 256, as said below
- expert_weight: bfloat16 [4, 7168, 4096], P('section', 'wide', 'narrow'), may hold values from -0.0625 to 0.0625
- expert_moment: float32 [4, 7168, 4096], P('section', 'wide', 'narrow'), may hold values from -6 to 6
- value_weight: bfloat16 [4, 4096, 1024], P('section', ('wide', 'narrow')), may hold values from -0.09375 to 0.09375
- value_moment: float32 [4, 4096, 1024], P('section', ('wide', 'narrow')), may hold values from -6 to 6
Outputs:
- expert_weight_next: bfloat16 [4, 7168, 4096], P('section', 'wide', 'narrow')
- expert_moment_next: float32 [4, 7168, 4096], P('section', 'wide', 'narrow')
- value_weight_next: bfloat16 [4, 4096, 1024], P('section', ('wide', 'narrow'))
- value_moment_next: float32 [4, 4096, 1024], P('section', ('wide', 'narrow'))
Inputs may be any that keep to these rules, and one draw needn't show every extreme that they name: The live slots of a micro-batch are slots 0 to slot_count - 1; in every layer and replica some micro-batch fills all 256 slots.
All inputs are finite; a program needn't handle non-finite values.
Results may differ from a plain program's by a relative error of at most 0.014.
Values may be sent and summed in bfloat16 or wider, within the bound.
A program may use at most 128 MiB of HBM per device.

v0:
```python
import math
import jax
import jax.numpy as jnp
from jax import lax
from jax.sharding import Mesh
from jax.sharding import PartitionSpec as P

D = 4096
FF = 7168
KV = 1024
WIDE = ("wide_0", "wide_1")
NARROW = ("narrow_0", "narrow_1")
WIDE_NARROW = ("wide_0", "wide_1", "narrow_0", "narrow_1")
SECTION_WIDE_NARROW = ("section", "wide_0", "wide_1", "narrow_0", "narrow_1")
MOMENTUM_DECAY = 0.9
STEP_RATE = 0.01


def over_axes(shard, axes):
    for axis in axes:
        shard = lax.psum(shard, axis)
    return shard


def on_device(
    normed_inputs,
    value_cotangent,
    expert_hidden,
    expert_cotangent,
    slot_gate,
    slot_count,
    expert_weight,
    expert_moment,
    value_weight,
    value_moment,
):
    input_rows = normed_inputs[0, 0].reshape(-1, normed_inputs.shape[-1])
    value_cot_rows = value_cotangent[0, 0].reshape(-1, value_cotangent.shape[-1])
    hidden_local = expert_hidden[0, 0]
    cotangent = expert_cotangent[0, 0]
    gate_local = slot_gate[0, 0]
    live_count = slot_count[0, 0]
    cot_piece = lax.all_gather(cotangent, WIDE, axis=1, tiled=True)
    gate_piece = lax.all_gather(gate_local, WIDE, axis=1, tiled=True)
    length = cot_piece.shape[1]
    positions = jnp.arange(length, dtype=jnp.int32)
    live = positions[None, :] < live_count[:, None]
    coefficient = jnp.where(
        live, gate_piece.astype(jnp.float32), jnp.zeros(gate_piece.shape, jnp.float32)
    )
    scaled = (coefficient[:, :, None] * cot_piece.astype(jnp.float32)).astype(jnp.bfloat16)
    summed = lax.dot_general(
        hidden_local, scaled, (((0, 1), (0, 1)), ((), ())), preferred_element_type=jnp.float32
    )
    expert_grad = lax.psum_scatter(
        summed.astype(jnp.bfloat16), NARROW, scatter_dimension=1, tiled=True
    ).astype(jnp.float32)
    value_grad = lax.psum_scatter(
        lax.dot_general(
            input_rows, value_cot_rows, (((0,), (0,)), ((), ())), preferred_element_type=jnp.float32
        ).astype(jnp.bfloat16),
        WIDE_NARROW,
        scatter_dimension=0,
        tiled=True,
    ).astype(jnp.float32)
    squares = jnp.sum(expert_grad * expert_grad) + jnp.sum(value_grad * value_grad)
    overall = over_axes(squares, SECTION_WIDE_NARROW)
    entry_count = lax.axis_size("section") * (FF * D + D * KV)
    factor = jnp.minimum(1.0, math.sqrt(entry_count) / jnp.sqrt(overall + 1e-06))
    expert_next = MOMENTUM_DECAY * expert_moment[0] + factor * expert_grad
    value_next = MOMENTUM_DECAY * value_moment[0] + factor * value_grad
    expert_weight_next = (expert_weight[0].astype(jnp.float32) - STEP_RATE * expert_next).astype(
        jnp.bfloat16
    )
    value_weight_next = (value_weight[0].astype(jnp.float32) - STEP_RATE * value_next).astype(
        jnp.bfloat16
    )
    return (expert_weight_next[None], expert_next[None], value_weight_next[None], value_next[None])


def solution(mesh):
    finer = Mesh(
        mesh.devices.reshape(mesh.shape["section"], 4, 2, 2, 2),
        ("section", "wide_0", "wide_1", "narrow_0", "narrow_1"),
    )
    in_specs = (
        P("section", NARROW, None, WIDE, None),
        P("section", NARROW, None, WIDE, None),
        P("section", NARROW, None, None, WIDE),
        P("section", NARROW, None, WIDE, None),
        P("section", NARROW, None, WIDE),
        P("section", NARROW, None),
        P("section", WIDE, NARROW),
        P("section", WIDE, NARROW),
        P("section", WIDE_NARROW, None),
        P("section", WIDE_NARROW, None),
    )
    out_specs = (
        P("section", WIDE, NARROW),
        P("section", WIDE, NARROW),
        P("section", WIDE_NARROW, None),
        P("section", WIDE_NARROW, None),
    )
    return jax.shard_map(
        on_device, mesh=finer, in_specs=in_specs, out_specs=out_specs, check_vma=False
    )
```

profile of v0, /device:TPU:1, one launch (start us, length us, event | category | flops | bytes accessed | tf_op | source)
XLA Modules:
  0.0 304.2 jit_solution(16088000934408733016)
XLA Ops:
  8.0 0.0 copy-start
  8.0 0.0 all-gather.4.cloned.1.call-start
  8.1 0.7 all-gather.4.cloned.1.call-update
  8.7 0.0 reduce-scatter.5.cloned.1.call-start
  8.8 1.1 copy-done
  9.9 7.9 %bitcast_convert_fusion = bf16[4096,1024]{1,0:T(8,128)(2,1)} fusion(bf16[1,1,4,96,4096]{4,3,2,1,0:T(8,128)(2,1)S(1)} %copy-done, bf16[1,1,4,96,1024]{4,3,2,1,0:T(8,128)(2,1)} %param.11), kind=kOutput, calls=%fused_computation.2 | convolution fusion | flops 3225419776 | bytes 12320768 | tf_op jit(solution)/shard_map/dot_general | solution.py:59
  17.8 0.0 copy-start.2
  17.8 0.0 copy-start.3
  17.8 0.0 reduce-scatter.5.cloned.1.call-update
  17.8 0.0 reduce-scatter.3.cloned.1.call-start
  17.8 0.6 copy-done.2
  18.4 0.1 copy.21
  18.6 31.8 %all-gather = bf16[1,1,4,256]{2,1,0,3:T(2,128)(2,1)S(1)} all-gather(bf16[1,1,4,32]{2,1,0,3:T(2,128)(2,1)S(1)} %copy.21), channel_id=2, replica_groups=mesh['section'=4,'wide_0'=4,'wide_1'=2,'narrow_0'=2,'narrow_1'=2] {'wide..., dimensions={3}, use_global_device_ids=true | all-gather | bytes 2304 | tf_op jit(solution)/shard_map/all_gather | solution.py:44
  50.3 0.1 convert_element_type.58
  50.5 0.0 copy-done.3
  50.5 0.1 copy.22
  50.6 70.8 %all-gather.4.cloned.1.call-done = bf16[1,1,4,256,4096]{4,3,2,1,0:T(8,128)(2,1)} async-done(((bf16[1,1,4,32,4096]{4,3,2,1,0:T(8,128)(2,1)}), bf16[1,1,4,256,4096]{4,3,2,1,0:T(8,128)(2,1)}) %all-gather.4.cloned.1.call-update) | async-done | bytes 8388624 | tf_op jit(solution)/shard_map/all_gather | solution.py:43
  121.4 14.1 %fusion.5 = bf16[896,4096]{0,1:T(8,128)(2,1)} fusion(bf16[1,1,4,256,4096]{4,3,2,1,0:T(8,128)(2,1)} %all-gather.4.cloned.1.call-done, f32[4,256]{1,0:T(4,128)S(1)} %copy.22, bf16[1,1,4,256,896]{4,3,2,1,0:T(8,128)(2,1)} %param.12), kind=kOutput, calls=%fused_computation.7 | convolution fusion | flops 7532445696 | bytes 17567744 | tf_op jit(solution)/shard_map/dot_general | solution.py:52
  135.6 0.0 reduce-scatter.3.cloned.1.call-update
  135.6 17.6 %reduce-scatter.5.cloned.1.call-done = bf16[128,1024]{1,0:T(8,128)(2,1)} async-done(((bf16[4096,1024]{1,0:T(8,128)(2,1)}), bf16[128,1024]{1,0:T(8,128)(2,1)}) %reduce-scatter.5.cloned.1.call-update) | async-done | bytes 262160 | tf_op jit(solution)/shard_map/reduce_scatter | solution.py:58
  153.2 1.7 fusion.16
  154.9 72.7 %reduce-scatter.3.cloned.1.call-done = bf16[896,1024]{0,1:T(8,128)(2,1)} async-done(((bf16[896,4096]{0,1:T(8,128)(2,1)}), bf16[896,1024]{0,1:T(8,128)(2,1)}) %reduce-scatter.3.cloned.1.call-update) | async-done | bytes 1835024 | tf_op jit(solution)/shard_map/reduce_scatter | solution.py:55
  227.6 3.0 %fusion.8 = f32[]{:T(128)} fusion(bf16[896,1024]{0,1:T(8,128)(2,1)} %reduce-scatter.3.cloned.1.call-done), kind=kLoop, calls=%fused_computation.10 | loop fusion | flops 2752511 | bytes 1835012 | tf_op jit(solution)/shard_map/reduce_sum | solution.py:66
  231.9 9.0 %psum.35 = f32[]{:T(128)} all-reduce(f32[]{:T(128)S(6)} %add.26), channel_id=1, replica_groups=mesh['section'=4,'wide_0'=4,'wide_1'=2,'narrow_0'=2,'narrow_1'=2] {'sect..., use_global_device_ids=true, to_apply=%region_4.5 | all-reduce | flops 1 | bytes 8 | tf_op jit(solution)/shard_map/psum | solution.py:21
  240.9 9.3 %psum.36 = f32[]{:T(128)} all-reduce(f32[]{:T(128)} %psum.35), channel_id=1, replica_groups=mesh['section'=4,'wide_0'=4,'wide_1'=2,'narrow_0'=2,'narrow_1'=2] {'wide..., use_global_device_ids=true, to_apply=%region_5.6 | all-reduce | flops 1 | bytes 8 | tf_op jit(solution)/shard_map/psum | solution.py:21
  250.2 5.9 %psum.37 = f32[]{:T(128)} all-reduce(f32[]{:T(128)} %psum.36), channel_id=1, replica_groups=mesh['section'=4,'wide_0'=4,'wide_1'=2,'narrow_0'=2,'narrow_1'=2] {'wide..., use_global_device_ids=true, to_apply=%region_6.7 | all-reduce | flops 1 | bytes 8 | tf_op jit(solution)/shard_map/psum | solution.py:21
  256.0 5.0 %copy.20 = f32[1,896,1024]{1,2,0:T(8,128)} copy(f32[1,896,1024]{2,1,0:T(8,128)} %param.17) | data formatting | bytes 7340032 | tf_op args[7]
  261.1 4.4 %psum.38 = f32[]{:T(128)} all-reduce(f32[]{:T(128)} %psum.37), channel_id=1, replica_groups=mesh['section'=4,'wide_0'=4,'wide_1'=2,'narrow_0'=2,'narrow_1'=2] {'narr..., use_global_device_ids=true, to_apply=%region_7.8 | all-reduce | flops 1 | bytes 8 | tf_op jit(solution)/shard_map/psum | solution.py:21
  265.4 3.8 %copy.19 = bf16[1,896,1024]{1,2,0:T(8,128)(2,1)} copy(bf16[1,896,1024]{2,1,0:T(8,128)(2,1)} %param.16) | data formatting | bytes 3670016 | tf_op args[6]
  269.2 9.4 %psum.39 = f32[]{:T(128)} all-reduce(f32[]{:T(128)} %psum.38), channel_id=1, replica_groups=mesh['section'=4,'wide_0'=4,'wide_1'=2,'narrow_0'=2,'narrow_1'=2] {'narr..., use_global_device_ids=true, to_apply=%region_8.9 | all-reduce | flops 1 | bytes 8 | tf_op jit(solution)/shard_map/psum | solution.py:21
  279.3 6.5 %fusion.12 = (f32[1,896,1024]{1,2,0:T(8,128)}, bf16[1,896,1024]{1,2,0:T(8,128)(2,1)}) fusion(bf16[896,1024]{0,1:T(8,128)(2,1)} %reduce-scatter.3.cloned.1.call-done, f32[1,896,1024]{1,2,0:T(8,128)} %copy.20, f32[]{:T(128)S(6)} %min_shard_map.3, bf16[1,896,1024]{1,2,0:T(8,128)(2,1)} %copy.19), kind=kLoop, calls=%fused_computation.15 | loop fusion | flops 7340032 | bytes 12845060 | tf_op jit(solution)/shard_map/broadcast_in_dim | solution.py:78
  285.8 3.8 %copy.24 = bf16[1,896,1024]{2,1,0:T(8,128)(2,1)} copy(bf16[1,896,1024]{1,2,0:T(8,128)(2,1)} %get-tuple-element.13) | data formatting | bytes 3670016
  289.6 0.0 copy-start.1
  289.6 5.0 %copy.25 = f32[1,896,1024]{2,1,0:T(8,128)} copy(f32[1,896,1024]{1,2,0:T(8,128)} %get-tuple-element.12) | data formatting | bytes 7340032
  294.6 0.0 copy-done.1
  294.6 2.1 fusion.19
  (1 shorter events, 0.0 us)
Async XLA Ops:
  8.0 1.9 copy-start
  8.0 113.4 %all-gather.4.cloned.1.call-start = ((), (), s32[]{:S(2)}) async-start(), calls=%async_computation.4 | async-start | bytes 9437184 | tf_op jit(solution)/shard_map/all_gather | solution.py:43
  8.7 144.4 %reduce-scatter.5.cloned.1.call-start = ((), (), s32[]{:S(2)}) async-start(), calls=%async_computation.3 | async-start | bytes 8650752 | tf_op jit(solution)/shard_map/reduce_scatter | solution.py:58
  17.8 0.7 copy-start.2
  17.8 32.7 %copy-start.3 = (s32[1,1,4]{2,1,0:T(1,128)S(1)}, s32[1,1,4]{2,1,0:T(1,128)}, u32[]{:S(2)}) copy-start(s32[1,1,4]{2,1,0:T(1,128)} %param.15) | copy-start | bytes 52
  17.8 209.8 %reduce-scatter.3.cloned.1.call-start = ((), (), s32[]{:S(2)}) async-start(), calls=%async_computation.2 | async-start | bytes 9175040 | tf_op jit(solution)/shard_map/reduce_scatter | solution.py:55
  289.6 5.0 %copy-start.1 = (bf16[128,1024]{1,0:T(8,128)(2,1)S(1)}, bf16[128,1024]{1,0:T(8,128)(2,1)}, u32[]{:S(2)}) copy-start(bf16[128,1024]{1,0:T(8,128)(2,1)} %reduce-scatter.5.cloned.1.call-done) | copy-start | bytes 786436
Sparse Core Ops, SparseCore 0:
  11.1 110.2 all-gather.3
Sparse Core Ops, SparseCore 1:
  17.9 135.2 reduce-scatter.4
  155.4 72.1 reduce-scatter.2
where the time goes:
time: 305 us; the launch traced here: 304 us
  waiting for transfers between devices  162 us (53%)
  blocking collectives  69.7 us (23%)
  matrix products  22 us (7%)
  local copies, waits for them, and re-layouts  19.5 us (6%)
  between operations  17.5 us (6%)
  other arithmetic  13.5 us (4%)
    reduce_scatter x1, waiting for transfers between devices, on_device(): lax.psum_scatter(summed.astype(jnp.bfloat16), NARROW, scatter_dimension=1...  72.7 us
    all_gather x1, waiting for transfers between devices, on_device(): cot_piece = lax.all_gather(cotangent, WIDE, axis=1, tiled=True)  70.8 us
    psum x5, blocking collectives, over_axes(): shard = lax.psum(shard, axis)  37.9 us
    all_gather x1, blocking collectives, on_device(): gate_piece = lax.all_gather(gate_local, WIDE, axis=1, tiled=True)  31.8 us
    unnamed x13, local copies, waits for them, and re-layouts  19.4 us
    reduce_scatter x1, waiting for transfers between devices, on_device(): lax.psum_scatter(lax.dot_general(input_rows, value_cot_rows, (((0,), (0,)...  17.6 us
    dot_general x1, matrix products, on_device(): lax.dot_general(hidden_local, scaled, (((0, 1), (0, 1)), ((), ())), prefe...  14.1 us
    dot_general x1, matrix products, on_device(): lax.dot_general(input_rows, value_cot_rows, (((0,), (0,)), ((), ())), pre...  7.87 us
  transfers between devices with their start and end apart: 3, of which 3 were waited for; matrix products, arithmetic and copies ran while one was open for 8% of the time, Pallas kernels for 0%

commit v1 on v0

--- a/solution.py
+++ b/solution.py
@@ -40,7 +40,8 @@
     cotangent = expert_cotangent[0, 0]
     gate_local = slot_gate[0, 0]
     live_count = slot_count[0, 0]
-    cot_piece = lax.all_gather(cotangent, WIDE, axis=1, tiled=True)
+    tiles = lax.all_gather(cotangent, WIDE)
+    cot_piece = jnp.concatenate(tiles, axis=1)
     gate_piece = lax.all_gather(gate_local, WIDE, axis=1, tiled=True)
     length = cot_piece.shape[1]
     positions = jnp.arange(length, dtype=jnp.int32)

time: 305 us -> 305 us (level)
  other arithmetic: 13.5 us -> 23.6 us
  waiting for transfers between devices: 162 us -> 152 us
    convert_element_type x0 -> x1, other arithmetic: none -> 10.1 us  [on_device(): (coefficient[:, :, None] * cot_piece.astype(jnp.float32)).astype(jnp.bflo...]
    reduce_scatter x1, waiting for transfers between devices: 17.6 us -> 7.71 us  [on_device(): lax.psum_scatter(lax.dot_general(input_rows, value_cot_rows, (((0,), (0,)...]
  transfers between devices with their start and end apart: 3 -> 3, of which waited for: 3 -> 3; matrix products, arithmetic and copies ran while one was open for 8% -> 11% of each run, Pallas kernels for 0% -> 0%
where the time goes in v1:
time: 305 us; the launch traced here: 304 us
  waiting for transfers between devices  152 us (50%)
  blocking collectives  69.7 us (23%)
  other arithmetic  23.6 us (8%)
  matrix products  21.8 us (7%)
  local copies, waits for them, and re-layouts  19.5 us (6%)
  between operations  17.5 us (6%)
    reduce_scatter x1, waiting for transfers between devices, on_device(): lax.psum_scatter(summed.astype(jnp.bfloat16), NARROW, scatter_dimension=1...  72.7 us
    all_gather x1, waiting for transfers between devices, on_device(): tiles = lax.all_gather(cotangent, WIDE)  70.8 us
    psum x5, blocking collectives, over_axes(): shard = lax.psum(shard, axis)  37.9 us
    all_gather x1, blocking collectives, on_device(): gate_piece = lax.all_gather(gate_local, WIDE, axis=1, tiled=True)  31.8 us
    unnamed x13, local copies, waits for them, and re-layouts  19.4 us
    dot_general x1, matrix products, on_device(): lax.dot_general(hidden_local, scaled, (((0, 1), (0, 1)), ((), ())), prefe...  13.9 us
    convert_element_type x1, other arithmetic, on_device(): (coefficient[:, :, None] * cot_piece.astype(jnp.float32)).astype(jnp.bflo...  10.1 us
    dot_general x1, matrix products, on_device(): lax.dot_general(input_rows, value_cot_rows, (((0,), (0,)), ((), ())), pre...  7.87 us
  transfers between devices with their start and end apart: 3, of which 3 were waited for; matrix products, arithmetic and copies ran while one was open for 11% of the time, Pallas kernels for 0%

profile of v1, /device:TPU:1, one launch (start us, length us, event | category | flops | bytes accessed | tf_op | source)
XLA Modules:
  0.0 304.2 jit_solution(6058906786890718244)
XLA Ops:
  8.0 0.0 copy-start
  8.0 0.0 all-gather.4.cloned.1.call-start
  8.1 0.7 all-gather.4.cloned.1.call-update
  8.7 0.0 reduce-scatter.5.cloned.1.call-start
  8.8 1.1 copy-done
  9.9 7.9 %bitcast_convert_fusion = bf16[4096,1024]{1,0:T(8,128)(2,1)} fusion(bf16[1,1,4,96,4096]{4,3,2,1,0:T(8,128)(2,1)S(1)} %copy-done, bf16[1,1,4,96,1024]{4,3,2,1,0:T(8,128)(2,1)} %param.11), kind=kOutput, calls=%fused_computation.3 | convolution fusion | flops 3225419776 | bytes 12320768 | tf_op jit(solution)/shard_map/dot_general | solution.py:60
  17.8 0.0 copy-start.2
  17.8 0.0 copy-start.3
  17.8 0.0 reduce-scatter.5.cloned.1.call-update
  17.8 0.0 reduce-scatter.3.cloned.1.call-start
  17.8 0.6 copy-done.2
  18.4 0.1 copy.27
  18.6 31.8 %all-gather = bf16[1,1,4,256]{2,1,0,3:T(2,128)(2,1)S(1)} all-gather(bf16[1,1,4,32]{2,1,0,3:T(2,128)(2,1)S(1)} %copy.27), channel_id=2, replica_groups=mesh['section'=4,'wide_0'=4,'wide_1'=2,'narrow_0'=2,'narrow_1'=2] {'wide..., dimensions={3}, use_global_device_ids=true | all-gather | bytes 2304 | tf_op jit(solution)/shard_map/all_gather | solution.py:45
  50.3 0.1 convert_element_type.68
  50.5 0.0 copy-done.3
  50.5 0.1 copy.28
  50.6 70.8 %all-gather.4.cloned.1.call-done = bf16[8,1,4,32,4096]{4,3,0,2,1:T(8,128)(2,1)} async-done(((bf16[1,1,4,32,4096]{4,3,0,2,1:T(8,128)(2,1)}), bf16[8,1,4,32,4096]{4,3,0,2,1:T(8,128)(2,1)}) %all-gather.4.cloned.1.call-update) | async-done | bytes 8388624 | tf_op jit(solution)/shard_map/all_gather | solution.py:43
  121.4 10.1 %fusion.1 = bf16[4,8,32,4096]{3,2,1,0:T(8,128)(2,1)} fusion(bf16[8,1,4,32,4096]{4,3,0,2,1:T(8,128)(2,1)} %all-gather.4.cloned.1.call-done, f32[4,8,32]{2,1,0:T(8,128)S(1)} %copy.28), kind=kLoop, calls=%fused_computation.2 | loop fusion | flops 12582912 | bytes 16781312 | tf_op jit(solution)/shard_map/convert_element_type | solution.py:52
  131.5 13.9 %fusion.2 = bf16[896,4096]{0,1:T(8,128)(2,1)} fusion(bf16[4,256,4096]{2,1,0:T(8,128)(2,1)} %bitcast.62, bf16[1,1,4,256,896]{4,3,2,1,0:T(8,128)(2,1)} %param.12), kind=kOutput, calls=%fused_computation.5 | convolution fusion | flops 7519862784 | bytes 17563648 | tf_op jit(solution)/shard_map/dot_general | solution.py:53
  145.4 0.0 reduce-scatter.3.cloned.1.call-update
  145.5 7.7 %reduce-scatter.5.cloned.1.call-done = bf16[128,1024]{1,0:T(8,128)(2,1)} async-done(((bf16[4096,1024]{1,0:T(8,128)(2,1)}), bf16[128,1024]{1,0:T(8,128)(2,1)}) %reduce-scatter.5.cloned.1.call-update) | async-done | bytes 262160 | tf_op jit(solution)/shard_map/reduce_scatter | solution.py:59
  153.2 1.7 fusion.11
  154.9 72.7 %reduce-scatter.3.cloned.1.call-done = bf16[896,1024]{0,1:T(8,128)(2,1)} async-done(((bf16[896,4096]{0,1:T(8,128)(2,1)}), bf16[896,1024]{0,1:T(8,128)(2,1)}) %reduce-scatter.3.cloned.1.call-update) | async-done | bytes 1835024 | tf_op jit(solution)/shard_map/reduce_scatter | solution.py:56
  227.6 3.0 %fusion.3 = f32[]{:T(128)} fusion(bf16[896,1024]{0,1:T(8,128)(2,1)} %reduce-scatter.3.cloned.1.call-done), kind=kLoop, calls=%fused_computation.8 | loop fusion | flops 2752511 | bytes 1835012 | tf_op jit(solution)/shard_map/reduce_sum | solution.py:67
  231.9 9.0 %psum.35 = f32[]{:T(128)} all-reduce(f32[]{:T(128)S(6)} %add.26), channel_id=1, replica_groups=mesh['section'=4,'wide_0'=4,'wide_1'=2,'narrow_0'=2,'narrow_1'=2] {'sect..., use_global_device_ids=true, to_apply=%region_4.5 | all-reduce | flops 1 | bytes 8 | tf_op jit(solution)/shard_map/psum | solution.py:21
  240.9 9.3 %psum.36 = f32[]{:T(128)} all-reduce(f32[]{:T(128)} %psum.35), channel_id=1, replica_groups=mesh['section'=4,'wide_0'=4,'wide_1'=2,'narrow_0'=2,'narrow_1'=2] {'wide..., use_global_device_ids=true, to_apply=%region_5.6 | all-reduce | flops 1 | bytes 8 | tf_op jit(solution)/shard_map/psum | solution.py:21
  250.2 5.9 %psum.37 = f32[]{:T(128)} all-reduce(f32[]{:T(128)} %psum.36), channel_id=1, replica_groups=mesh['section'=4,'wide_0'=4,'wide_1'=2,'narrow_0'=2,'narrow_1'=2] {'wide..., use_global_device_ids=true, to_apply=%region_6.7 | all-reduce | flops 1 | bytes 8 | tf_op jit(solution)/shard_map/psum | solution.py:21
  256.0 3.8 %copy.25 = bf16[1,896,1024]{1,2,0:T(8,128)(2,1)} copy(bf16[1,896,1024]{2,1,0:T(8,128)(2,1)} %param.16) | data formatting | bytes 3670016 | tf_op args[6]
  259.8 4.4 %psum.38 = f32[]{:T(128)} all-reduce(f32[]{:T(128)} %psum.37), channel_id=1, replica_groups=mesh['section'=4,'wide_0'=4,'wide_1'=2,'narrow_0'=2,'narrow_1'=2] {'narr..., use_global_device_ids=true, to_apply=%region_7.8 | all-reduce | flops 1 | bytes 8 | tf_op jit(solution)/shard_map/psum | solution.py:21
  264.2 5.0 %copy.26 = f32[1,896,1024]{1,2,0:T(8,128)} copy(f32[1,896,1024]{2,1,0:T(8,128)} %param.17) | data formatting | bytes 7340032 | tf_op args[7]
  269.2 9.4 %psum.39 = f32[]{:T(128)} all-reduce(f32[]{:T(128)} %psum.38), channel_id=1, replica_groups=mesh['section'=4,'wide_0'=4,'wide_1'=2,'narrow_0'=2,'narrow_1'=2] {'narr..., use_global_device_ids=true, to_apply=%region_8.9 | all-reduce | flops 1 | bytes 8 | tf_op jit(solution)/shard_map/psum | solution.py:21
  279.3 6.5 %fusion.7 = (f32[1,896,1024]{1,2,0:T(8,128)}, bf16[1,896,1024]{1,2,0:T(8,128)(2,1)}) fusion(bf16[896,1024]{0,1:T(8,128)(2,1)} %reduce-scatter.3.cloned.1.call-done, f32[1,896,1024]{1,2,0:T(8,128)} %copy.26, f32[]{:T(128)S(6)} %min_shard_map.3, bf16[1,896,1024]{1,2,0:T(8,128)(2,1)} %copy.25), kind=kLoop, calls=%fused_computation.13 | loop fusion | flops 7340032 | bytes 12845060 | tf_op jit(solution)/shard_map/broadcast_in_dim | solution.py:79
  285.8 5.0 %copy.32 = f32[1,896,1024]{2,1,0:T(8,128)} copy(f32[1,896,1024]{1,2,0:T(8,128)} %get-tuple-element.16) | data formatting | bytes 7340032
  290.8 0.0 copy-start.1
  290.8 3.8 %copy.31 = bf16[1,896,1024]{2,1,0:T(8,128)(2,1)} copy(bf16[1,896,1024]{1,2,0:T(8,128)(2,1)} %get-tuple-element.17) | data formatting | bytes 3670016
  294.6 0.0 copy-done.1
  294.6 2.1 fusion.14
  (1 shorter events, 0.0 us)
Async XLA Ops:
  8.0 1.9 copy-start
  8.0 113.4 %all-gather.4.cloned.1.call-start = ((), (), s32[]{:S(2)}) async-start(), calls=%async_computation.4 | async-start | bytes 9437184 | tf_op jit(solution)/shard_map/all_gather | solution.py:43
  8.7 144.4 %reduce-scatter.5.cloned.1.call-start = ((), (), s32[]{:S(2)}) async-start(), calls=%async_computation.3 | async-start | bytes 8650752 | tf_op jit(solution)/shard_map/reduce_scatter | solution.py:59
  17.8 0.7 copy-start.2
  17.8 32.7 %copy-start.3 = (s32[1,1,4]{2,1,0:T(1,128)S(1)}, s32[1,1,4]{2,1,0:T(1,128)}, u32[]{:S(2)}) copy-start(s32[1,1,4]{2,1,0:T(1,128)} %param.15) | copy-start | bytes 52
  17.8 209.8 %reduce-scatter.3.cloned.1.call-start = ((), (), s32[]{:S(2)}) async-start(), calls=%async_computation.2 | async-start | bytes 9175040 | tf_op jit(solution)/shard_map/reduce_scatter | solution.py:56
  290.8 3.8 %copy-start.1 = (bf16[128,1024]{1,0:T(8,128)(2,1)S(1)}, bf16[128,1024]{1,0:T(8,128)(2,1)}, u32[]{:S(2)}) copy-start(bf16[128,1024]{1,0:T(8,128)(2,1)} %reduce-scatter.5.cloned.1.call-done) | copy-start | bytes 786436
Sparse Core Ops, SparseCore 0:
  11.1 110.2 all-gather.3
Sparse Core Ops, SparseCore 1:
  17.9 135.2 reduce-scatter.4
  155.4 72.1 reduce-scatter.2
